TPU v7x, 16 devices: a whole 2x2x2 slice. The times are simulated.
16 devices in a mesh: data: 16 (over z, y, x, core).
Axes of the slice: x: 2, y: 2, z: 2, core: 2. Of those that a mesh axis runs over, the one named last changes fastest.
Arguments:
- grad_qkv: bfloat16 [16, 3, 1769472], P('data')
- weight_qkv: float32 [3, 1769472], P(None, 'data')
- mom_qkv: float32 [3, 1769472], P(None, 'data')
- var_qkv: float32 [3, 1769472], P(None, 'data')
- grad_proj: bfloat16 [16, 3, 589824], P('data')
- weight_proj: float32 [3, 589824], P(None, 'data')
- mom_proj: float32 [3, 589824], P(None, 'data')
- var_proj: float32 [3, 589824], P(None, 'data')
- grad_fc_in: bfloat16 [16, 3, 2359296], P('data')
- weight_fc_in: float32 [3, 2359296], P(None, 'data')
- mom_fc_in: float32 [3, 2359296], P(None, 'data')
- var_fc_in: float32 [3, 2359296], P(None, 'data')
- grad_fc_out: bfloat16 [16, 3, 2359296], P('data')
- weight_fc_out: float32 [3, 2359296], P(None, 'data')
- mom_fc_out: float32 [3, 2359296], P(None, 'data')
- var_fc_out: float32 [3, 2359296], P(None, 'data')
Outputs:
- output 1: bfloat16 [3, 1769472], replicated
- output 2: float32 [3, 1769472], P(None, 'data')
- output 3: float32 [3, 1769472], P(None, 'data')
- output 4: float32 [3, 1769472], P(None, 'data')
- output 5: bfloat16 [3, 589824], replicated
- output 6: float32 [3, 589824], P(None, 'data')
- output 7: float32 [3, 589824], P(None, 'data')
- output 8: float32 [3, 589824], P(None, 'data')
- output 9: bfloat16 [3, 2359296], replicated
- output 10: float32 [3, 2359296], P(None, 'data')
- output 11: float32 [3, 2359296], P(None, 'data')
- output 12: float32 [3, 2359296], P(None, 'data')
- output 13: bfloat16 [3, 2359296], replicated
- output 14: float32 [3, 2359296], P(None, 'data')
- output 15: float32 [3, 2359296], P(None, 'data')
- output 16: float32 [3, 2359296], P(None, 'data')
All inputs are finite; a program needn't handle non-finite values.
Results may differ from a plain program's by a relative error of at most 0.001.
Values are sent between devices in bfloat16 or wider.
A program may use at most 1 GiB of HBM per device.

v0:
```python
import jax
import jax.numpy as jnp
from jax import lax
from jax.sharding import PartitionSpec as P

STEP = 10
LEARN_RATE = 0.1
BETA_ONE = 0.9
BETA_TWO = 0.999
EPSILON = 1e-6
WEIGHT_DECAY = 0.01


def solution(mesh):
    groups = mesh.shape["data"]
    grad_spec = P("data", None, None)
    shard_spec = P(None, "data")
    full_spec = P(None, None)

    def lamb_tensor(local_grad, weight, first_mom, second_mom):
        layers = local_grad.shape[1]
        pieces = local_grad.reshape(layers, groups, local_grad.shape[2] // groups)
        received = lax.all_to_all(pieces, "data", 1, 1, tiled=True)
        grad_mean = jnp.sum(received, axis=1, dtype=jnp.float32) / groups
        new_first = BETA_ONE * first_mom + (1.0 - BETA_ONE) * grad_mean
        new_second = BETA_TWO * second_mom + (1.0 - BETA_TWO) * grad_mean * grad_mean
        direction = (new_first / (1.0 - BETA_ONE ** STEP)) / (jnp.sqrt(new_second / (1.0 - BETA_TWO ** STEP)) + EPSILON) + WEIGHT_DECAY * weight
        part_sums = jnp.stack([jnp.sum(weight * weight, axis=1), jnp.sum(direction * direction, axis=1)])
        norm_pair = jnp.sqrt(lax.psum(part_sums, "data"))
        trust_ratio = (norm_pair[0] / norm_pair[1])[:, None]
        new_weight = weight - LEARN_RATE * trust_ratio * direction
        replica = lax.all_gather(new_weight.astype(jnp.bfloat16), "data", axis=1, tiled=True)
        return replica, new_weight, new_first, new_second

    def device_step(*blocks):
        results = []
        for kind_pos in range(len(blocks) // 4):
            first_pos = 4 * kind_pos
            results.extend(lamb_tensor(blocks[first_pos], blocks[first_pos + 1], blocks[first_pos + 2], blocks[first_pos + 3]))
        return tuple(results)

    return jax.shard_map(device_step, mesh=mesh, in_specs=(grad_spec, shard_spec, shard_spec, shard_spec) * 4, out_specs=(full_spec, shard_spec, shard_spec, shard_spec) * 4, check_vma=False)
```

profile of v0, /device:TPU:0, one launch (start us, length us, event | category | flops | bytes accessed | tf_op | source)
XLA Modules:
  0.0 1050.6 jit_solution(9628001516197635859)
XLA Ops:
  7.2 60.8 %all_to_all.20 = bf16[3,16,36864]{2,0,1:T(4,128)(2,1)} all-to-all(bf16[3,16,36864]{2,0,1:T(4,128)(2,1)} %bitcast.27), channel_id=1, replica_groups=mesh['data'=16] {'data'}, dimensions={1} | all-to-all | bytes 7077888 | tf_op jit(solution)/shard_map/all_to_all | solution.py:23
  68.1 162.4 %all_to_all.21 = bf16[3,16,110592]{2,0,1:T(4,128)(2,1)} all-to-all(bf16[3,16,110592]{2,0,1:T(4,128)(2,1)} %bitcast.26), channel_id=1, replica_groups=mesh['data'=16] {'data'}, dimensions={1} | all-to-all | bytes 21233664 | tf_op jit(solution)/shard_map/all_to_all | solution.py:23
  230.5 209.6 %all_to_all.22 = bf16[3,16,147456]{2,0,1:T(4,128)(2,1)} all-to-all(bf16[3,16,147456]{2,0,1:T(4,128)(2,1)S(1)} %bitcast.22), channel_id=1, replica_groups=mesh['data'=16] {'data'}, dimensions={1} | all-to-all | bytes 28311552 | tf_op jit(solution)/shard_map/all_to_all | solution.py:23
  440.1 4.0 all-to-all-start.3
  444.1 0.0 all-gather.7.cloned.1.call-start
  444.2 4.5 convert_reduce_fusion.3
  448.8 2.2 multiply_reduce_fusion.6
  451.0 11.5 %convert_reduce_fusion.2 = f32[3,110592]{1,0:T(4,128)S(1)} fusion(bf16[3,16,110592]{2,0,1:T(4,128)(2,1)} %all_to_all.21), kind=kLoop, calls=%fused_computation.2 | loop fusion | flops 10285056 | bytes 11943936 | tf_op jit(solution)/shard_map/reduce_sum | solution.py:24
  462.5 5.0 multiply_reduce_fusion.4
  467.6 10.3 convert_reduce_fusion.1
  477.9 8.2 multiply_reduce_fusion.2
  486.2 182.1 %all-to-all-done.3 = bf16[3,16,147456]{2,0,1:T(4,128)(2,1)} async-done(((bf16[3,16,147456]{2,0,1:T(4,128)(2,1)}), bf16[3,16,147456]{2,0,1:T(4,128)(2,1)}, u32[]{:S(2)}, u32[]{:S(2)}) %all-to-all-start.3) | async-done | bytes 14155808 | tf_op jit(solution)/shard_map/all_to_all | solution.py:23
  668.3 9.9 convert_reduce_fusion
  678.3 8.1 multiply_reduce_fusion
  686.4 33.8 %all-reduce = (f32[2,3]{1,0:T(2,128)}, f32[2,3]{1,0:T(2,128)}, f32[2,3]{1,0:T(2,128)}, f32[2,3]{1,0:T(2,128)}) all-reduce(f32[2,3]{1,0:T(2,128)S(1)} %get-tuple-element.48, f32[2,3]{1,0:T(2,128)S(1)} %get-tuple-element.49, f32[2,3]{1,0:T(2,128)S(1)} %get-tuple-element.50, ...), channel_id=1, replica_groups=mesh['data'=16] {'data'}, use_global_device_ids=true, to_apply=%region_3.0 | all-reduce | flops 24 | bytes 192 | tf_op jit(solution)/shard_map/psum | solution.py:29
  720.2 0.7 sqrt.25
  720.9 0.7 sqrt.27
  721.6 1.2 fusion.2
  722.8 0.3 all-gather.5.cloned.1.call-start
  723.1 4.2 fusion.3
  727.4 0.0 all-gather.9.cloned.1.call-start
  727.4 3.5 fusion.1
  731.0 0.0 all-gather.11.cloned.1.call-start
  731.1 4.0 fusion
  735.1 25.8 %all-gather.7.cloned.1.call-done = bf16[3,589824]{1,0:T(4,128)(2,1)} async-done(((bf16[3,36864]{1,0:T(4,128)(2,1)}), bf16[3,589824]{1,0:T(4,128)(2,1)}) %all-gather.7.cloned.1.call-update) | async-done | bytes 3538960 | tf_op jit(solution)/shard_map/all_gather | solution.py:32
  760.9 70.6 %all-gather.5.cloned.1.call-done = bf16[3,1769472]{1,0:T(4,128)(2,1)} async-done(((bf16[3,110592]{1,0:T(4,128)(2,1)}), bf16[3,1769472]{1,0:T(4,128)(2,1)}) %all-gather.5.cloned.1.call-update) | async-done | bytes 10616848 | tf_op jit(solution)/shard_map/all_gather | solution.py:32
  831.5 86.1 %all-gather.9.cloned.1.call-done = bf16[3,2359296]{1,0:T(4,128)(2,1)} async-done(((bf16[3,147456]{1,0:T(4,128)(2,1)}), bf16[3,2359296]{1,0:T(4,128)(2,1)}) %all-gather.9.cloned.1.call-update) | async-done | bytes 14155792 | tf_op jit(solution)/shard_map/all_gather | solution.py:32
  917.6 85.9 %all-gather.11.cloned.1.call-done = bf16[3,2359296]{1,0:T(4,128)(2,1)} async-done(((bf16[3,147456]{1,0:T(4,128)(2,1)}), bf16[3,2359296]{1,0:T(4,128)(2,1)}) %all-gather.11.cloned.1.call-update) | async-done | bytes 14155792 | tf_op jit(solution)/shard_map/all_gather | solution.py:32
  1003.5 12.6 %copy.36 = bf16[3,1769472]{1,0:T(4,128)(2,1)} copy(bf16[3,1769472]{1,0:T(4,128)(2,1)} %all-gather.5.cloned.1.call-done) | data formatting | bytes 21233664
  1016.2 7.9 copy.37
  1024.1 6.9 copy.38
  1031.0 13.1 %copy.39 = bf16[3,2359296]{1,0:T(4,128)(2,1)} copy(bf16[3,2359296]{1,0:T(4,128)(2,1)} %all-gather.11.cloned.1.call-done) | data formatting | bytes 28311552
  (60 shorter events, 0.3 us)
Async XLA Ops:
  7.2 223.3 %slice-start = ((s8[18874368]{0:T(1024)(128)(4,1)}), s8[4194304]{0:T(1024)(128)(4,1)S(1)}, s32[]{:S(2)}) async-start(s8[18874368]{0:T(1024)(128)(4,1)} %bitcast.20), calls=%async_computation.8 | async-start | bytes 8388608
  7.2 223.3 %slice-start.1 = ((s8[18874368]{0:T(1024)(128)(4,1)}), s8[4194304]{0:T(1024)(128)(4,1)S(1)}, s32[]{:S(2)}) async-start(s8[18874368]{0:T(1024)(128)(4,1)} %bitcast.20), calls=%async_computation.9 | async-start | bytes 8388608
  68.0 162.4 %slice-start.2 = ((s8[18874368]{0:T(1024)(128)(4,1)}), s8[4194304]{0:T(1024)(128)(4,1)S(1)}, s32[]{:S(2)}) async-start(s8[18874368]{0:T(1024)(128)(4,1)} %bitcast.20), calls=%async_computation.10 | async-start | bytes 8388608
  68.0 162.4 %slice-start.3 = ((s8[18874368]{0:T(1024)(128)(4,1)}), s8[4194304]{0:T(1024)(128)(4,1)S(1)}, s32[]{:S(2)}) async-start(s8[18874368]{0:T(1024)(128)(4,1)} %bitcast.20), calls=%async_computation.11 | async-start | bytes 8388608
  68.0 162.4 %slice-start.4 = ((s8[18874368]{0:T(1024)(128)(4,1)}), s8[2097152]{0:T(1024)(128)(4,1)S(1)}, s32[]{:S(2)}) async-start(s8[18874368]{0:T(1024)(128)(4,1)} %bitcast.20), calls=%async_computation.12 | async-start | bytes 4194304
  440.1 228.2 %all-to-all-start.3 = ((bf16[3,16,147456]{2,0,1:T(4,128)(2,1)}), bf16[3,16,147456]{2,0,1:T(4,128)(2,1)}, u32[]{:S(2)}, u32[]{:S(2)}) async-start(bf16[3,16,147456]{2,0,1:T(4,128)(2,1)} %bitcast.23), calls=%async_computation.3 | async-start | bytes 37748736 | tf_op jit(solution)/shard_map/all_to_all | solution.py:23
  444.1 4.6 copy-start.3
  444.1 4.6 copy-start.7
  444.1 4.6 copy-start.8
  444.1 316.8 %all-gather.7.cloned.1.call-start = ((), (), s32[]{:S(2)}) async-start(), calls=%async_computation.5 | async-start | bytes 5013504 | tf_op jit(solution)/shard_map/all_gather | solution.py:32
  451.0 11.5 %copy-start.2 = (f32[3,110592]{1,0:T(4,128)S(1)}, f32[3,110592]{1,0:T(4,128)}, u32[]{:S(2)}) copy-start(f32[3,110592]{1,0:T(4,128)} %param.17) | copy-start | bytes 3981316
  451.0 11.5 %copy-start.5 = (f32[3,110592]{1,0:T(4,128)S(1)}, f32[3,110592]{1,0:T(4,128)}, u32[]{:S(2)}) copy-start(f32[3,110592]{1,0:T(4,128)} %param.18) | copy-start | bytes 3981316
  451.0 11.5 %copy-start.6 = (f32[3,110592]{1,0:T(4,128)S(1)}, f32[3,110592]{1,0:T(4,128)}, u32[]{:S(2)}) copy-start(f32[3,110592]{1,0:T(4,128)} %param.19) | copy-start | bytes 3981316
  467.5 10.4 copy-start
  467.5 10.4 copy-start.4
  668.3 10.0 copy-start.1
  678.3 8.1 copy-start.9
  678.3 8.1 copy-start.10
  722.8 108.7 %all-gather.5.cloned.1.call-start = ((), (), s32[]{:S(2)}) async-start(), calls=%async_computation.4 | async-start | bytes 15040512 | tf_op jit(solution)/shard_map/all_gather | solution.py:32
  723.1 4.2 copy-start.12
  723.1 4.2 copy-start.11
  727.4 190.2 %all-gather.9.cloned.1.call-start = ((), (), s32[]{:S(2)}) async-start(), calls=%async_computation.6 | async-start | bytes 20054016 | tf_op jit(solution)/shard_map/all_gather | solution.py:32
  731.0 272.5 %all-gather.11.cloned.1.call-start = ((), (), s32[]{:S(2)}) async-start(), calls=%async_computation.7 | async-start | bytes 20054016 | tf_op jit(solution)/shard_map/all_gather | solution.py:32
  1003.5 20.6 %slice-start.5 = ((s8[18874368]{0:T(1024)(128)(4,1)}), s8[4194304]{0:T(1024)(128)(4,1)S(1)}, s32[]{:S(2)}) async-start(s8[18874368]{0:T(1024)(128)(4,1)} %bitcast.24), calls=%async_computation.13 | async-start | bytes 8388608
  1003.5 20.6 %slice-start.6 = ((s8[18874368]{0:T(1024)(128)(4,1)}), s8[4194304]{0:T(1024)(128)(4,1)S(1)}, s32[]{:S(2)}) async-start(s8[18874368]{0:T(1024)(128)(4,1)} %bitcast.24), calls=%async_computation.14 | async-start | bytes 8388608
  1003.5 20.6 %slice-start.7 = ((s8[18874368]{0:T(1024)(128)(4,1)}), s8[4194304]{0:T(1024)(128)(4,1)S(1)}, s32[]{:S(2)}) async-start(s8[18874368]{0:T(1024)(128)(4,1)} %bitcast.24), calls=%async_computation.15 | async-start | bytes 8388608
  1003.5 20.6 %slice-start.8 = ((s8[18874368]{0:T(1024)(128)(4,1)}), s8[4194304]{0:T(1024)(128)(4,1)S(1)}, s32[]{:S(2)}) async-start(s8[18874368]{0:T(1024)(128)(4,1)} %bitcast.24), calls=%async_computation.16 | async-start | bytes 8388608
  1016.2 8.0 slice-start.9
Sparse Core Ops, SparseCore 0:
  723.0 37.9 all-gather.6
  763.7 67.7 all-gather.4
  834.3 83.2 all-gather.8
  920.2 83.2 all-gather.10
where the time goes:
time: 1050 us
  blocking collectives  467 us (44%)
  waiting for transfers between devices  451 us (43%)
  other arithmetic  72.8 us (7%)
  local copies, waits for them, and re-layouts  42 us (4%)
  between operations  14.1 us (1%)
    all_to_all x3, blocking collectives, lamb_tensor(): received = lax.all_to_all(pieces, 'data', 1, 1, tiled=True)  433 us
    all_gather x4, waiting for transfers between devices, lamb_tensor(): lax.all_gather(new_weight.astype(jnp.bfloat16), 'data', axis=1, tiled=True)  268 us
    all_to_all x1, waiting for transfers between devices, lamb_tensor(): received = lax.all_to_all(pieces, 'data', 1, 1, tiled=True)  182 us
    unnamed x50, local copies, waits for them, and re-layouts  40.6 us
    reduce_sum x4, other arithmetic, lamb_tensor(): grad_mean = jnp.sum(received, axis=1, dtype=jnp.float32) / groups  36.3 us
    psum x1, blocking collectives, lamb_tensor(): norm_pair = jnp.sqrt(lax.psum(part_sums, 'data'))  33.8 us
    reduce_sum x4, other arithmetic, lamb_tensor(): jnp.sum(direction * direction, axis=1)  23.5 us
  transfers between devices with their start and end apart: 5, of which 5 were waited for; matrix products, arithmetic and copies ran while one was open for 5% of the time, Pallas kernels for 0%

commit v1 on v0

v1 whole, which is shorter than its diff:
```python
import functools

import jax
import jax.numpy as jnp
from jax import lax
from jax.experimental import pallas as pl
from jax.experimental.pallas import tpu as pltpu
from jax.sharding import PartitionSpec as P


STEP = 10
LEARN_RATE = 0.1
BETA_ONE = 0.9
BETA_TWO = 0.999
EPSILON = 1e-6
WEIGHT_DECAY = 0.01

MESH = pl.DeviceIdType.MESH
CHUNK = 12288
INNER = 1024
ORDERS = ((0, 1, 2), (1, 2, 0), (2, 0, 1))


def direction_of(grad_mean, weight, first_mom, second_mom):
    new_first = BETA_ONE * first_mom + (1.0 - BETA_ONE) * grad_mean
    new_second = BETA_TWO * second_mom + (1.0 - BETA_TWO) * grad_mean * grad_mean
    direction = (new_first / (1.0 - BETA_ONE ** STEP)) / (jnp.sqrt(new_second / (1.0 - BETA_TWO ** STEP)) + EPSILON) + WEIGHT_DECAY * weight
    return new_first, new_second, direction


def reduce_kernel(width, g_ref, w_ref, m_ref, v_ref, mean_ref, ratio_ref,
                  own, peer, pair, send1, keep, recv1, recv2, recv3, mean, wv, mv, vv, acc, part, parts, ratio,
                  own_sem, peer_send, peer_recv, s1, r1, s2, r2, s3, r3, state_sem, mean_sem, part_send, part_recv, ratio_sem):
    chunks = width // CHUNK
    me = lax.axis_index("data")
    core = me % 2
    bits = ((me // 2) % 2, (me // 4) % 2, (me // 8) % 2)
    partner = me + 1 - 2 * core
    neighbour = tuple(me + (2 << d) * (1 - 2 * bits[d]) for d in range(3))

    def shard_start(rel, parity):
        owner = parity
        for d in range(3):
            bit = (rel >> d) & 1
            owner = owner + (2 << d) * (1 - bits[d] if bit else bits[d])
        return owner * width

    def columns(rel, parity, t):
        return pl.ds(pl.multiple_of(shard_start(rel, parity) + t * CHUNK, 128), CHUNK)

    def load_own(t, rel):
        return pltpu.make_async_copy(g_ref.at[:, columns(rel, core, t)], own.at[t, rel], own_sem.at[t])

    def give_peer(t, rel):
        return pltpu.make_async_remote_copy(
            src_ref=g_ref.at[:, columns(rel, 1 - core, t)], dst_ref=peer.at[t, rel],
            send_sem=peer_send.at[t], recv_sem=peer_recv.at[t], device_id=(partner,), device_id_type=MESH)

    def stage(src, dst, ssem, rsem, dim):
        return pltpu.make_async_remote_copy(src_ref=src, dst_ref=dst, send_sem=ssem, recv_sem=rsem,
                                            device_id=(neighbour[dim],), device_id_type=MESH)

    def local_loop(t, _):
        for rel in range(8):
            load_own(t, rel).start()
        return 0

    lax.fori_loop(0, chunks, local_loop, 0)
    states = [pltpu.make_async_copy(src, dst, state_sem.at[i]) for i, (src, dst) in enumerate(((w_ref, wv), (m_ref, mv), (v_ref, vv)))]
    for copy in states:
        copy.start()
    barrier = pltpu.get_barrier_semaphore()
    for k in range(1, 16):
        pl.semaphore_signal(barrier, inc=1, device_id=((me + k) % 16,), device_id_type=MESH)
    pl.semaphore_wait(barrier, 15)

    def peer_loop(t, _):
        for rel in range(8):
            give_peer(t, rel).start()
        return 0

    lax.fori_loop(0, chunks, peer_loop, 0)
    acc[...] = jnp.zeros_like(acc)
    for copy in states:
        copy.wait()

    def pair_stage(t):
        pltpu.make_async_copy(own.at[t], own.at[t], own_sem.at[t]).wait()
        pltpu.make_async_copy(peer.at[t], peer.at[t], peer_recv.at[t]).wait()
        for rel in range(8):
            def inner(i, _, rel=rel):
                cols = pl.ds(pl.multiple_of(i * INNER, INNER), INNER)
                pair[rel] = own[t, rel, :, cols].astype(jnp.float32) + peer[t, rel, :, cols].astype(jnp.float32)
                for row in range(3):
                    a, b, c = ((rel >> d) & 1 for d in ORDERS[row])
                    dst = send1 if a else keep
                    dst[t, row, 2 * b + c, :, cols] = pair[rel, row:row + 1, :]
                return 0

            lax.fori_loop(0, CHUNK // INNER, inner, 0)
        for row in range(3):
            stage(send1.at[t, row], recv1.at[t, row], s1.at[t], r1.at[t], ORDERS[row][0]).start()

    def add_stage(t, recv, rsem, count):
        pltpu.make_async_copy(recv.at[t], recv.at[t], rsem.at[t]).wait()

        def inner(i, _):
            cols = pl.ds(pl.multiple_of(i * INNER, INNER), INNER)
            for row in range(3):
                for k in range(count):
                    keep[t, row, k, :, cols] = keep[t, row, k, :, cols] + recv[t, row, k, :, cols]
            return 0

        lax.fori_loop(0, CHUNK // INNER, inner, 0)

    def mean_copy(t):
        cols = pl.ds(pl.multiple_of(t * CHUNK, CHUNK), CHUNK)
        return pltpu.make_async_copy(mean.at[t], mean_ref.at[:, cols], mean_sem.at[t])

    def last_stage(t):
        pltpu.make_async_copy(recv3.at[t], recv3.at[t], r3.at[t]).wait()

        def inner(i, _):
            cols = pl.ds(pl.multiple_of(i * INNER, INNER), INNER)
            state_cols = pl.ds(pl.multiple_of(t * CHUNK + i * INNER, INNER), INNER)
            for row in range(3):
                total = (keep[t, row, 0, :, cols] + recv3[t, row, 0, :, cols]) / 16
                mean[t, row:row + 1, cols] = total
                weight = wv[row:row + 1, state_cols]
                direction = direction_of(total, weight, mv[row:row + 1, state_cols], vv[row:row + 1, state_cols])[2]
                acc[row] += weight * weight
                acc[3 + row] += direction * direction
            return 0

        lax.fori_loop(0, CHUNK // INNER, inner, 0)
        mean_copy(t).start()

    def step(t, _):
        @pl.when(t < chunks)
        def _():
            pair_stage(t)

        @pl.when((t >= 1) & (t < chunks + 1))
        def _():
            u = t - 1
            add_stage(u, recv1, r1, 4)
            for row in range(3):
                stage(keep.at[u, row, pl.ds(2, 2)], recv2.at[u, row], s2.at[u], r2.at[u], ORDERS[row][1]).start()

        @pl.when((t >= 2) & (t < chunks + 2))
        def _():
            u = t - 2
            add_stage(u, recv2, r2, 2)
            for row in range(3):
                stage(keep.at[u, row, pl.ds(1, 1)], recv3.at[u, row], s3.at[u], r3.at[u], ORDERS[row][2]).start()

        @pl.when(t >= 3)
        def _():
            last_stage(t - 3)

        return 0

    lax.fori_loop(0, chunks + 3, step, 0)

    for j in range(6):
        part[j:j + 1, :] = jnp.broadcast_to(jnp.sum(acc[j], axis=1, keepdims=True), (1, 128))
    for j in range(6, 8):
        part[j:j + 1, :] = jnp.zeros((1, 128), jnp.float32)
    parts[me] = part[...]
    shares = [pltpu.make_async_remote_copy(src_ref=part, dst_ref=parts.at[me], send_sem=part_send.at[k], recv_sem=part_recv.at[k],
                                           device_id=((me + k + 1) % 16,), device_id_type=MESH) for k in range(15)]
    for copy in shares:
        copy.start()

    def drain(t, _):
        pltpu.make_async_copy(peer.at[t], peer.at[t], peer_send.at[t]).wait()
        pltpu.make_async_copy(send1.at[t], send1.at[t], s1.at[t]).wait()
        pltpu.make_async_copy(recv2.at[t], recv2.at[t], s2.at[t]).wait()
        pltpu.make_async_copy(recv3.at[t], recv3.at[t], s3.at[t]).wait()
        mean_copy(t).wait()
        return 0

    lax.fori_loop(0, chunks, drain, 0)
    for copy in shares:
        copy.wait()
    total = parts[0]
    for i in range(1, 16):
        total = total + parts[i]
    norms = jnp.sqrt(total)
    ratio[...] = norms[0:3, :] / norms[3:6, :]
    copy = pltpu.make_async_copy(ratio, ratio_ref, ratio_sem)
    copy.start()
    copy.wait()


def reduce_and_norms(local_grad, weight, first_mom, second_mom, number):
    layers, width = weight.shape
    chunks = width // CHUNK
    f32, bf16 = jnp.float32, jnp.bfloat16
    dma = pltpu.SemaphoreType.DMA
    any_space = pl.BlockSpec(memory_space=pl.ANY)
    return pl.pallas_call(
        functools.partial(reduce_kernel, width),
        out_shape=(jax.ShapeDtypeStruct((layers, width), f32), jax.ShapeDtypeStruct((layers, 128), f32)),
        in_specs=[any_space] * 4,
        out_specs=(any_space, any_space),
        scratch_shapes=[
            pltpu.VMEM((chunks, 8, 3, CHUNK), bf16), pltpu.VMEM((chunks, 8, 3, CHUNK), bf16), pltpu.VMEM((8, 3, INNER), f32),
            pltpu.VMEM((chunks, 3, 4, 1, CHUNK), f32), pltpu.VMEM((chunks, 3, 4, 1, CHUNK), f32),
            pltpu.VMEM((chunks, 3, 4, 1, CHUNK), f32), pltpu.VMEM((chunks, 3, 2, 1, CHUNK), f32), pltpu.VMEM((chunks, 3, 1, 1, CHUNK), f32),
            pltpu.VMEM((chunks, 3, CHUNK), f32),
            pltpu.VMEM((3, width), f32), pltpu.VMEM((3, width), f32), pltpu.VMEM((3, width), f32),
            pltpu.VMEM((6, 1, INNER), f32), pltpu.VMEM((8, 128), f32), pltpu.VMEM((16, 8, 128), f32), pltpu.VMEM((3, 128), f32),
            dma((chunks,)), dma((chunks,)), dma((chunks,)),
            dma((chunks,)), dma((chunks,)), dma((chunks,)), dma((chunks,)), dma((chunks,)), dma((chunks,)),
            dma((3,)), dma((chunks,)), dma((15,)), dma((15,)), dma,
        ],
        compiler_params=pltpu.CompilerParams(collective_id=number, has_side_effects=True, vmem_limit_bytes=67043328),
        cost_estimate=pl.CostEstimate(flops=int(width * 2e6), bytes_accessed=width * 3 * 16 * 2, transcendentals=0),
    )(local_grad, weight, first_mom, second_mom)


def solution(mesh):
    grad_spec = P("data", None, None)
    shard_spec = P(None, "data")
    full_spec = P(None, None)

    def device_step(*blocks):
        results = [None] * 16
        last = None
        for number, kind in enumerate((2, 3, 0, 1)):
            local_grad, weight, first_mom, second_mom = blocks[4 * kind:4 * kind + 4]
            grad = local_grad.reshape(local_grad.shape[1:])
            if last is not None:
                grad = lax.optimization_barrier((grad, last))[0]
            mean, ratio = reduce_and_norms(grad, weight, first_mom, second_mom, number)
            new_first, new_second, direction = direction_of(mean, weight, first_mom, second_mom)
            new_weight = weight - LEARN_RATE * ratio[:, :1] * direction
            rounded = new_weight.astype(jnp.bfloat16)
            last = rounded
            replica = lax.all_gather(rounded, "data", axis=1, tiled=True)
            results[4 * kind:4 * kind + 4] = [replica, new_weight, new_first, new_second]
        return tuple(results)

    return jax.shard_map(device_step, mesh=mesh, in_specs=(grad_spec, shard_spec, shard_spec, shard_spec) * 4, out_specs=(full_spec, shard_spec, shard_spec, shard_spec) * 4, check_vma=False)
```

time: 1050 us -> 695 us (0.66)
  blocking collectives: 467 us -> 0 us
  Pallas kernels: 0 us -> 331 us
  waiting for transfers between devices: 451 us -> 279 us
  other arithmetic: 72.8 us -> 29.9 us
    all_to_all x3 -> x0, blocking collectives: 433 us -> none  [lamb_tensor(): received = lax.all_to_all(pieces, 'data', 1, 1, tiled=True)]
    pallas_call x0 -> x4, Pallas kernels: none -> 331 us  [reduce_and_norms(): pl.pallas_call(functools.partial(reduce_kernel, width), out_shape=(jax.Sh...]
    all_to_all x1 -> x0, waiting for transfers between devices: 182 us -> none  [lamb_tensor(): received = lax.all_to_all(pieces, 'data', 1, 1, tiled=True)]
    reduce_sum x8 -> x0, other arithmetic: 59.8 us -> none  [the longest x4 36.3 us: lamb_tensor(): grad_mean = jnp.sum(received, axis=1, dtype=jnp.float32) / groups]
    psum x1 -> x0, blocking collectives: 33.8 us -> none  [lamb_tensor(): norm_pair = jnp.sqrt(lax.psum(part_sums, 'data'))]
    convert_element_type x4, other arithmetic: 12.9 us -> 26.8 us  [device_step(): rounded = new_weight.astype(jnp.bfloat16)]
    unnamed x50 -> x14, local copies, waits for them, and re-layouts: 40.6 us -> 40.5 us
  transfers between devices with their start and end apart: 5 -> 4, of which waited for: 5 -> 4; matrix products, arithmetic and copies ran while one was open for 5% -> 0% of each run, Pallas kernels for 0% -> 0%
where the time goes in v1:
time: 695 us
  Pallas kernels  331 us (48%)
  waiting for transfers between devices  279 us (40%)
  local copies, waits for them, and re-layouts  40.5 us (6%)
  other arithmetic  29.9 us (4%)
  between operations  13.8 us (2%)
    pallas_call x4, Pallas kernels, reduce_and_norms(): pl.pallas_call(functools.partial(reduce_kernel, width), out_shape=(jax.Sh...  331 us
    all_gather x4, waiting for transfers between devices, device_step(): replica = lax.all_gather(rounded, 'data', axis=1, tiled=True)  277 us
    unnamed x14, local copies, waits for them, and re-layouts  40.5 us
    convert_element_type x4, other arithmetic, device_step(): rounded = new_weight.astype(jnp.bfloat16)  26.8 us
  transfers between devices with their start and end apart: 4, of which 4 were waited for; matrix products, arithmetic and copies ran while one was open for 0% of the time, Pallas kernels for 0%

profile of v1, /device:TPU:0, one launch (start us, length us, event | category | flops | bytes accessed | tf_op | source)
XLA Modules:
  0.0 694.7 jit_solution(8510891584015686914)
XLA Ops:
  7.2 0.0 all-gather.7.cloned.1.call-start
  7.2 108.1 %shard_map.279 = (f32[3,147456]{1,0:T(4,128)}, f32[3,128]{1,0:T(4,128)}) custom-call(bf16[3,2359296]{1,0:T(4,128)(2,1)} %bitcast.6, f32[3,147456]{1,0:T(4,128)} %w_ref.4, f32[3,147456]{1,0:T(4,128)} %m_ref.4, f32[3,147456]{1,0:T(4,128)} %v_ref.4), custom_call_target="tpu_custom_call" | custom-call | flops 294912000000 | bytes 14155776 | tf_op jit(solution)/shard_map/pallas_call | solution.py:202
  115.3 0.8 multiply_reduce_fusion.3
  116.1 8.2 %fusion.10 = (bf16[3,147456]{1,0:T(4,128)(2,1)}, f32[3,147456]{1,0:T(4,128)}, f32[3,147456]{1,0:T(4,128)}, f32[3,147456]{1,0:T(4,128)}) fusion(f32[3,147456]{1,0:T(4,128)} %w_ref.4, f32[3]{0:T(128)S(1)} %multiply_reduce_fusion.3, f32[3,147456]{1,0:T(4,128)} %get-tuple-element.28, f32[3,147456]{1,0:T(4,128)} %m_ref.4, f32[3,147456]{1,0:T(4,128)} %v_ref.4), kind=kLoop, calls=%fused_computation.23 | loop fusion | flops 7077888 | bytes 13271052 | tf_op jit(solution)/shard_map/convert_element_type | solution.py:239
  124.3 105.0 %shard_map.280 = (f32[3,147456]{1,0:T(4,128)}, f32[3,128]{1,0:T(4,128)}) custom-call(bf16[3,2359296]{1,0:T(4,128)(2,1)} %bitcast.7, f32[3,147456]{1,0:T(4,128)} %w_ref.5, f32[3,147456]{1,0:T(4,128)} %m_ref.5, f32[3,147456]{1,0:T(4,128)} %v_ref.5), custom_call_target="tpu_custom_call" | custom-call | flops 294912000000 | bytes 14155776 | tf_op jit(solution)/shard_map/pallas_call | solution.py:202
  229.3 0.8 multiply_reduce_fusion.2
  230.1 8.2 %fusion.8 = (bf16[3,147456]{1,0:T(4,128)(2,1)}, f32[3,147456]{1,0:T(4,128)}, f32[3,147456]{1,0:T(4,128)}, f32[3,147456]{1,0:T(4,128)}) fusion(f32[3,147456]{1,0:T(4,128)} %w_ref.5, f32[3]{0:T(128)S(1)} %multiply_reduce_fusion.2, f32[3,147456]{1,0:T(4,128)} %get-tuple-element.31, f32[3,147456]{1,0:T(4,128)} %m_ref.5, f32[3,147456]{1,0:T(4,128)} %v_ref.5), kind=kLoop, calls=%fused_computation.22 | loop fusion | flops 7077888 | bytes 13271052 | tf_op jit(solution)/shard_map/convert_element_type | solution.py:239
  238.3 82.0 %shard_map.281 = (f32[3,110592]{1,0:T(4,128)}, f32[3,128]{1,0:T(4,128)}) custom-call(bf16[3,1769472]{1,0:T(4,128)(2,1)} %bitcast.8, f32[3,110592]{1,0:T(4,128)} %w_ref.6, f32[3,110592]{1,0:T(4,128)} %m_ref.6, f32[3,110592]{1,0:T(4,128)} %v_ref.6), custom_call_target="tpu_custom_call" | custom-call | flops 221184000000 | bytes 10616832 | tf_op jit(solution)/shard_map/pallas_call | solution.py:202
  320.3 0.8 multiply_reduce_fusion.1
  321.1 6.5 fusion.6
  327.6 36.3 %shard_map.282 = (f32[3,36864]{1,0:T(4,128)}, f32[3,128]{1,0:T(4,128)}) custom-call(bf16[3,589824]{1,0:T(4,128)(2,1)} %bitcast.9, f32[3,36864]{1,0:T(4,128)} %w_ref.7, f32[3,36864]{1,0:T(4,128)} %m_ref.7, f32[3,36864]{1,0:T(4,128)} %v_ref.7), custom_call_target="tpu_custom_call" | custom-call | flops 73728000000 | bytes 3538944 | tf_op jit(solution)/shard_map/pallas_call | solution.py:202
  363.9 0.8 multiply_reduce_fusion
  364.7 3.8 fusion.4
  368.5 0.0 all-gather.7.cloned.1.call-update
  368.5 0.0 all-gather.5.cloned.1.call-start
  368.5 0.7 all-gather.5.cloned.1.call-update
  369.2 0.0 all-gather.9.cloned.1.call-start
  369.3 0.7 all-gather.9.cloned.1.call-update
  370.0 0.0 all-gather.11.cloned.1.call-start
  370.0 0.5 all-gather.11.cloned.1.call-update
  370.5 34.5 %all-gather.7.cloned.1.call-done = bf16[3,589824]{1,0:T(4,128)(2,1)} async-done(((bf16[3,36864]{1,0:T(4,128)(2,1)}), bf16[3,589824]{1,0:T(4,128)(2,1)}) %all-gather.7.cloned.1.call-update) | async-done | bytes 3538960 | tf_op jit(solution)/shard_map/all_gather | solution.py:241
  405.1 70.6 %all-gather.5.cloned.1.call-done = bf16[3,1769472]{1,0:T(4,128)(2,1)} async-done(((bf16[3,110592]{1,0:T(4,128)(2,1)}), bf16[3,1769472]{1,0:T(4,128)(2,1)}) %all-gather.5.cloned.1.call-update) | async-done | bytes 10616848 | tf_op jit(solution)/shard_map/all_gather | solution.py:241
  475.7 86.1 %all-gather.9.cloned.1.call-done = bf16[3,2359296]{1,0:T(4,128)(2,1)} async-done(((bf16[3,147456]{1,0:T(4,128)(2,1)}), bf16[3,2359296]{1,0:T(4,128)(2,1)}) %all-gather.9.cloned.1.call-update) | async-done | bytes 14155792 | tf_op jit(solution)/shard_map/all_gather | solution.py:241
  561.7 85.9 %all-gather.11.cloned.1.call-done = bf16[3,2359296]{1,0:T(4,128)(2,1)} async-done(((bf16[3,147456]{1,0:T(4,128)(2,1)}), bf16[3,2359296]{1,0:T(4,128)(2,1)}) %all-gather.11.cloned.1.call-update) | async-done | bytes 14155792 | tf_op jit(solution)/shard_map/all_gather | solution.py:241
  647.7 12.6 %copy.36 = bf16[3,1769472]{1,0:T(4,128)(2,1)} copy(bf16[3,1769472]{1,0:T(4,128)(2,1)} %all-gather.5.cloned.1.call-done) | data formatting | bytes 21233664
  660.3 7.9 %copy.37 = bf16[3,589824]{1,0:T(4,128)(2,1)} copy(bf16[3,589824]{1,0:T(4,128)(2,1)} %all-gather.7.cloned.1.call-done) | data formatting | bytes 7077888
  668.2 0.0 slice-done
  668.2 0.0 slice-done.1
  668.2 0.0 slice-done.2
  668.2 0.0 slice-done.3
  668.3 6.9 copy.38
  675.1 13.1 %copy.39 = bf16[3,2359296]{1,0:T(4,128)(2,1)} copy(bf16[3,2359296]{1,0:T(4,128)(2,1)} %all-gather.11.cloned.1.call-done) | data formatting | bytes 28311552
  (7 shorter events, 0.0 us)
Async XLA Ops:
  7.2 397.9 %all-gather.7.cloned.1.call-start = ((), (), s32[]{:S(2)}) async-start(), calls=%async_computation.1 | async-start | bytes 5013504 | tf_op jit(solution)/shard_map/all_gather | solution.py:241
  368.5 107.2 %all-gather.5.cloned.1.call-start = ((), (), s32[]{:S(2)}) async-start(), calls=%async_computation | async-start | bytes 15040512 | tf_op jit(solution)/shard_map/all_gather | solution.py:241
  369.2 192.5 %all-gather.9.cloned.1.call-start = ((), (), s32[]{:S(2)}) async-start(), calls=%async_computation.2 | async-start | bytes 20054016 | tf_op jit(solution)/shard_map/all_gather | solution.py:241
  370.0 277.7 %all-gather.11.cloned.1.call-start = ((), (), s32[]{:S(2)}) async-start(), calls=%async_computation.3 | async-start | bytes 20054016 | tf_op jit(solution)/shard_map/all_gather | solution.py:241
  647.6 20.6 %slice-start = ((s8[18874368]{0:T(1024)(128)(4,1)}), s8[4194304]{0:T(1024)(128)(4,1)S(1)}, s32[]{:S(2)}) async-start(s8[18874368]{0:T(1024)(128)(4,1)} %bitcast.4), calls=%async_computation.4 | async-start | bytes 8388608
  647.6 20.6 %slice-start.1 = ((s8[18874368]{0:T(1024)(128)(4,1)}), s8[4194304]{0:T(1024)(128)(4,1)S(1)}, s32[]{:S(2)}) async-start(s8[18874368]{0:T(1024)(128)(4,1)} %bitcast.4), calls=%async_computation.5 | async-start | bytes 8388608
  647.6 20.6 %slice-start.2 = ((s8[18874368]{0:T(1024)(128)(4,1)}), s8[4194304]{0:T(1024)(128)(4,1)S(1)}, s32[]{:S(2)}) async-start(s8[18874368]{0:T(1024)(128)(4,1)} %bitcast.4), calls=%async_computation.6 | async-start | bytes 8388608
  647.6 20.6 %slice-start.3 = ((s8[18874368]{0:T(1024)(128)(4,1)}), s8[4194304]{0:T(1024)(128)(4,1)S(1)}, s32[]{:S(2)}) async-start(s8[18874368]{0:T(1024)(128)(4,1)} %bitcast.4), calls=%async_computation.7 | async-start | bytes 8388608
  660.3 8.0 %slice-start.4 = ((s8[18874368]{0:T(1024)(128)(4,1)}), s8[2097152]{0:T(1024)(128)(4,1)S(1)}, s32[]{:S(2)}) async-start(s8[18874368]{0:T(1024)(128)(4,1)} %bitcast.4), calls=%async_computation.8 | async-start | bytes 4194304
Sparse Core Ops, SparseCore 0:
  368.6 36.4 all-gather.6
  407.9 67.7 all-gather.4
  478.5 83.2 all-gather.8
  564.4 83.2 all-gather.10
